TPU v7x, 16 devices: a 4x2x1 block of a 4x4x8 slice. The times are simulated.
16 devices in a mesh: rep: 2 (over y, z), pp: 8 (over x, core).
Axes of the slice: x: 4, y: 2, z: 1, core: 2. Of those that a mesh axis runs over, the one named last changes fastest.
The devices are a block of a 4x4x8 slice.
Arguments:
- x: bfloat16 [32, 512, 640], P('rep'), parts along dimension 0
- dy: bfloat16 [32, 512, 640], P('rep'), parts along dimension 0
- w_gate: bfloat16 [8, 640, 1536], P('pp')
- w_up: bfloat16 [8, 640, 1536], P('pp')
- w_down: bfloat16 [8, 1536, 640], P('pp')
Outputs:
- output 1: bfloat16 [16, 640, 1536], P(('rep', 'pp')), parts along dimension 0
- output 2: bfloat16 [16, 640, 1536], P(('rep', 'pp')), parts along dimension 0
- output 3: bfloat16 [16, 1536, 640], P(('rep', 'pp')), parts along dimension 0
There are 2 independent parts. A program takes and returns all parts, laid end to end along the dimension named above; an argument that names none is the same for every part.
All inputs are finite; a program needn't handle non-finite values.
Results may differ from a plain program's by a relative error of at most 0.0307.
Values are sent between devices in bfloat16 or wider.
A program may use at most 768 MiB of HBM per device.

v0:
```python
import jax
import jax.numpy as jnp
from jax import lax
from jax.sharding import PartitionSpec as P

NAMES = ("w_gate", "w_up", "w_down")


def matmul(a, w):
    return jnp.dot(a, w, preferred_element_type=jnp.float32).astype(jnp.bfloat16)


def normed(h):
    wide = h.astype(jnp.float32)
    scale = lax.rsqrt(jnp.mean(wide**2, -1, keepdims=True) + 1e-6)
    return (wide * scale).astype(jnp.bfloat16)


def layer(h, w):
    a = normed(h)
    gate = jnp.dot(a, w["w_gate"], preferred_element_type=jnp.float32)
    up = jnp.dot(a, w["w_up"], preferred_element_type=jnp.float32)
    return h + matmul((jax.nn.silu(gate) * up).astype(jnp.bfloat16), w["w_down"])


def stage(weights, h):
    for number in range(weights["w_gate"].shape[0]):
        h = layer(h, {name: w[number] for name, w in weights.items()})
    return h


def solution(mesh):
    stages = mesh.shape["pp"]
    onward = [(i, i + 1) for i in range(stages - 1)]
    back_again = [(i + 1, i) for i in range(stages - 1)]

    def step(x, dy, *arrays):
        weights = dict(zip(NAMES, arrays, strict=True))
        micro, me = x.shape[0], lax.axis_index("pp")
        kept, came = jnp.zeros_like(x), jnp.zeros_like(x[0])
        for t in range(micro + stages - 1):
            number = jnp.clip(t - me, 0, micro - 1)
            at_work = (t >= me) & (t - me < micro)
            h = jnp.where(me == 0, x[min(t, micro - 1)], came)
            was = lax.dynamic_index_in_dim(kept, number, 0, keepdims=False)
            kept = lax.dynamic_update_index_in_dim(kept, jnp.where(at_work, h, was), number, 0)
            came = lax.ppermute(stage(weights, h), "pp", onward)
        total = {name: jnp.zeros(w.shape, jnp.float32) for name, w in weights.items()}
        came, behind = jnp.zeros_like(x[0]), stages - 1 - me
        for t in range(micro + stages - 1):
            number = jnp.clip(t - behind, 0, micro - 1)
            at_work = (t >= behind) & (t - behind < micro)
            by_y = jnp.where(behind == 0, dy[min(t, micro - 1)], came)
            _, back = jax.vjp(stage, weights, lax.dynamic_index_in_dim(kept, number, 0, keepdims=False))
            by_w, by_h = back(by_y)
            total = {name: total[name] + jnp.where(at_work, by_w[name].astype(jnp.float32), 0.0) for name in NAMES}
            came = lax.ppermute(by_h, "pp", back_again)
        return tuple(total[name].astype(jnp.bfloat16) for name in NAMES)

    return jax.shard_map(
        step,
        mesh=mesh,
        in_specs=(P("rep", None, None),) * 2 + (P("pp", None, None),) * 3,
        out_specs=(P(("rep", "pp"), None, None),) * 3,
        check_vma=False,
    )
```

profile of v0, /device:TPU:112, one launch (start us, length us, event | category | flops | bytes accessed | tf_op | source)
XLA Modules:
  0.0 1219.6 jit_solution(8787754723255585360)
XLA Ops:
  26.4 10.4 collective-permute-start.1
  48.8 10.5 collective-permute-start.2
  71.8 10.2 collective-permute-start.3
  94.9 10.2 collective-permute-start.4
  112.2 6.9 fusion.926
  119.1 10.7 collective-permute-start.5
  136.4 6.9 fusion.923
  143.3 10.3 collective-permute-start.6
  160.5 6.9 fusion.920
  167.5 10.2 collective-permute-start.7
  184.7 6.9 fusion.917
  191.7 10.4 collective-permute-start.8
  208.9 6.9 fusion.914
  215.8 10.3 collective-permute-start.9
  233.1 6.9 fusion.911
  240.0 11.1 collective-permute-start.10
  263.8 6.9 fusion.908
  287.8 6.9 fusion.905
  333.4 6.7 fusion.899
  357.2 7.0 fusion.896
  381.6 7.0 fusion.893
  406.3 7.0 fusion.890
  429.7 6.7 fusion.887
  452.8 6.7 fusion.884
  477.1 7.0 fusion.881
  500.4 6.7 fusion.878
  681.6 8.3 collective-permute-done.25
  707.3 7.4 collective-permute-done.26
  732.0 7.6 collective-permute-done.27
  757.2 7.7 collective-permute-done.28
  782.6 7.5 collective-permute-done.29
  807.5 7.7 collective-permute-done.30
  832.7 7.6 collective-permute-done.31
  858.0 7.5 collective-permute-done.32
  882.9 7.7 collective-permute-done.33
  908.3 7.6 collective-permute-done.34
  933.5 7.5 collective-permute-done.35
  958.5 7.7 collective-permute-done.36
  983.8 7.7 collective-permute-done.37
  1009.0 7.5 collective-permute-done.38
  1033.9 7.7 collective-permute-done.39
  1059.2 7.6 collective-permute-done.40
  1084.4 7.5 collective-permute-done.41
  1109.4 7.7 collective-permute-done.42
  1141.0 7.7 collective-permute-done.43
  1151.3 21.6 %fusion.94 = bf16[1,640,1536]{2,1,0:T(8,128)(2,1)} fusion(bf16[512,1536]{1,0:T(8,128)(2,1)} %convolution_convert_fusion.69, bf16[640,1536]{1,0:T(8,128)(2,1)} %convolution_convert_fusion.1, bf16[640,1536]{1,0:T(8,128)(2,1)} %convolution_convert_fusion.2, bf16[640,1536]{1,0:T(8,128)(2,1)} %convolution_convert_fusion.3, ...), kind=kOutput, calls=%fused_computation.325 | convolution fusion | flops 1081147392 | bytes 50595868 | tf_op jit(solution)/shard_map/transpose(jvp())/dot_general | solution.py:22
  1173.0 23.4 %fusion.96 = bf16[1,640,1536]{2,1,0:T(8,128)(2,1)} fusion(f32[512,1536]{1,0:T(8,128)} %fusion.278, f32[512,1536]{1,0:T(8,128)} %fusion.188, bf16[512,1536]{1,0:T(8,128)(2,1)} %convolution_convert_fusion.69, bf16[640,1536]{1,0:T(8,128)(2,1)} %convolution_convert_fusion.24, bf16[640,1536]{1,0:T(8,128)(2,1)} %convolution_convert_fusion.25, ...), kind=kOutput, calls=%fused_computation.327 | convolution fusion | flops 1085079552 | bytes 53741596 | tf_op jit(solution)/shard_map/transpose(jvp())/dot_general | solution.py:21
  1196.4 22.7 %fusion.95 = bf16[1,1536,640]{2,1,0:T(8,128)(2,1)} fusion(bf16[1536,640]{1,0:T(8,128)(2,1)} %convolution_convert_fusion.47, bf16[1536,640]{1,0:T(8,128)(2,1)} %convolution_convert_fusion.48, bf16[1536,640]{1,0:T(8,128)(2,1)} %convolution_convert_fusion.49, bf16[1536,640]{1,0:T(8,128)(2,1)} %convolution_convert_fusion.50, ...), kind=kOutput, calls=%fused_computation.326 | convolution fusion | flops 1080492032 | bytes 52822040 | tf_op jit(solution)/shard_map/transpose(jvp())/dot_general | solution.py:10
  (715 shorter events, 788.4 us)
Async XLA Ops:
  12.6 3.4 collective-permute-start
  26.4 12.1 collective-permute-start.1
  48.8 11.9 collective-permute-start.2
  71.8 11.9 collective-permute-start.3
  94.9 11.9 collective-permute-start.4
  119.1 11.9 collective-permute-start.5
  143.3 11.9 collective-permute-start.6
  167.5 11.9 collective-permute-start.7
  191.7 11.9 collective-permute-start.8
  215.8 11.9 collective-permute-start.9
  240.0 18.5 %collective-permute-start.10 = (bf16[512,640]{1,0:T(8,128)(2,1)}, bf16[512,640]{1,0:T(8,128)(2,1)}, u32[]{:S(2)}, u32[]{:S(2)}) collective-permute-start(bf16[512,640]{1,0:T(8,128)(2,1)} %fusion.911), channel_id=1, source_target_pairs={{0,1},{1,2},{2,3},{3,4},{4,5},{5,6},{6,7},{8,9},{9,10},{10,11},{11... | collective-permute-start | bytes 1966088 | tf_op jit(solution)/shard_map/ppermute | solution.py:47
  270.8 11.7 collective-permute-start.11
  294.7 10.6 collective-permute-start.12
  316.5 12.4 %collective-permute-start.13 = (bf16[512,640]{1,0:T(8,128)(2,1)}, bf16[512,640]{1,0:T(8,128)(2,1)S(1)}, u32[]{:S(2)}, u32[]{:S(2)}) collective-permute-start(bf16[512,640]{1,0:T(8,128)(2,1)} %fusion.902), channel_id=1, source_target_pairs={{0,1},{1,2},{2,3},{3,4},{4,5},{5,6},{6,7},{8,9},{9,10},{10,11},{11... | collective-permute-start | bytes 1966088 | tf_op jit(solution)/shard_map/ppermute | solution.py:47
  340.1 11.7 collective-permute-start.14
  364.2 12.0 collective-permute-start.15
  388.6 12.3 %collective-permute-start.16 = (bf16[512,640]{1,0:T(8,128)(2,1)}, bf16[512,640]{1,0:T(8,128)(2,1)S(1)}, u32[]{:S(2)}, u32[]{:S(2)}) collective-permute-start(bf16[512,640]{1,0:T(8,128)(2,1)} %fusion.893), channel_id=1, source_target_pairs={{0,1},{1,2},{2,3},{3,4},{4,5},{5,6},{6,7},{8,9},{9,10},{10,11},{11... | collective-permute-start | bytes 1966088 | tf_op jit(solution)/shard_map/ppermute | solution.py:47
  413.2 11.9 collective-permute-start.17
  436.3 12.0 collective-permute-start.18
  459.5 12.3 %collective-permute-start.19 = (bf16[512,640]{1,0:T(8,128)(2,1)}, bf16[512,640]{1,0:T(8,128)(2,1)S(1)}, u32[]{:S(2)}, u32[]{:S(2)}) collective-permute-start(bf16[512,640]{1,0:T(8,128)(2,1)} %fusion.884), channel_id=1, source_target_pairs={{0,1},{1,2},{2,3},{3,4},{4,5},{5,6},{6,7},{8,9},{9,10},{10,11},{11... | collective-permute-start | bytes 1966088 | tf_op jit(solution)/shard_map/ppermute | solution.py:47
  484.1 11.7 collective-permute-start.20
  507.1 11.5 collective-permute-start.21
  546.0 49.4 %copy-start.67 = (f32[512]{0:T(512)}, f32[512]{0:T(512)S(1)}, u32[]{:S(2)}) copy-start(f32[512]{0:T(512)S(1)} %fusion.1379) | copy-start | bytes 6148
  546.1 46.0 %copy-start.69 = (f32[512]{0:T(512)}, f32[512]{0:T(512)S(1)}, u32[]{:S(2)}) copy-start(f32[512]{0:T(512)S(1)} %fusion.1378) | copy-start | bytes 6148
  546.1 42.9 %copy-start.71 = (f32[512]{0:T(512)}, f32[512]{0:T(512)S(1)}, u32[]{:S(2)}) copy-start(f32[512]{0:T(512)S(1)} %fusion.1377) | copy-start | bytes 6148
  546.1 39.7 %copy-start.73 = (f32[512]{0:T(512)}, f32[512]{0:T(512)S(1)}, u32[]{:S(2)}) copy-start(f32[512]{0:T(512)S(1)} %fusion.1376) | copy-start | bytes 6148
  547.0 54.5 %collective-permute-start.22 = (bf16[512,640]{1,0:T(8,128)(2,1)S(1)}, bf16[512,640]{1,0:T(8,128)(2,1)S(1)}, u32[]{:S(2)}, u32[]{:S(2)}) collective-permute-start(bf16[512,640]{1,0:T(8,128)(2,1)S(1)} %fusion.1099), channel_id=1, source_target_pairs={{1,0},{2,1},{3,2},{4,3},{5,4},{6,5},{7,6},{9,8},{10,9},{11,10},{12... | collective-permute-start | bytes 1966088 | tf_op jit(solution)/shard_map/ppermute | solution.py:57
  615.0 13.9 %collective-permute-start.23 = (bf16[512,640]{1,0:T(8,128)(2,1)S(1)}, bf16[512,640]{1,0:T(8,128)(2,1)S(1)}, u32[]{:S(2)}, u32[]{:S(2)}) collective-permute-start(bf16[512,640]{1,0:T(8,128)(2,1)S(1)} %fusion.1098), channel_id=1, source_target_pairs={{1,0},{2,1},{3,2},{4,3},{5,4},{6,5},{7,6},{9,8},{10,9},{11,10},{12... | collective-permute-start | bytes 1966088 | tf_op jit(solution)/shard_map/ppermute | solution.py:57
  650.1 8.9 collective-permute-start.24
  677.3 12.7 %collective-permute-start.25 = (bf16[512,640]{1,0:T(8,128)(2,1)S(1)}, bf16[512,640]{1,0:T(8,128)(2,1)S(1)}, u32[]{:S(2)}, u32[]{:S(2)}) collective-permute-start(bf16[512,640]{1,0:T(8,128)(2,1)S(1)} %fusion.1096), channel_id=1, source_target_pairs={{1,0},{2,1},{3,2},{4,3},{5,4},{6,5},{7,6},{9,8},{10,9},{11,10},{12... | collective-permute-start | bytes 1966088 | tf_op jit(solution)/shard_map/ppermute | solution.py:57
  702.8 11.9 collective-permute-start.26
  727.7 11.9 collective-permute-start.27
  752.9 11.9 collective-permute-start.28
  778.1 11.9 collective-permute-start.29
  803.3 11.9 collective-permute-start.30
  828.5 11.9 collective-permute-start.31
  853.6 11.9 collective-permute-start.32
  878.7 11.9 collective-permute-start.33
  904.0 11.9 collective-permute-start.34
  929.1 11.9 collective-permute-start.35
  954.3 11.9 collective-permute-start.36
  979.5 11.9 collective-permute-start.37
  1004.6 11.9 collective-permute-start.38
  1029.7 11.9 collective-permute-start.39
  1054.8 11.9 collective-permute-start.40
  1080.0 11.9 collective-permute-start.41
  1105.1 11.9 collective-permute-start.42
  1136.7 11.9 collective-permute-start.43
  (130 other events, 737.5 us)
where the time goes:
time: 1240 us; the launch traced here: 1220 us
  matrix products  714 us (58%)
  starting transfers between devices  201 us (16%)
  waiting for transfers between devices  164 us (13%)
  other arithmetic  79.6 us (6%)
  local copies, waits for them, and re-layouts  56.6 us (5%)
    dot_general x68, matrix products, matmul(): jnp.dot(a, w, preferred_element_type=jnp.float32).astype(jnp.bfloat16)  276 us
    dot_general x90, matrix products, layer(): gate = jnp.dot(a, w['w_gate'], preferred_element_type=jnp.float32)  242 us
    dot_general x68, matrix products, layer(): up = jnp.dot(a, w['w_up'], preferred_element_type=jnp.float32)  197 us
    ppermute x22, starting transfers between devices, step(): came = lax.ppermute(stage(weights, h), 'pp', onward)  167 us
    ppermute x22, waiting for transfers between devices, step(): came = lax.ppermute(by_h, 'pp', back_again)  148 us
    dynamic_update_slice x23, other arithmetic, step(): lax.dynamic_update_index_in_dim(kept, jnp.where(at_work, h, was), number, 0)  35.6 us
    ppermute x22, starting transfers between devices, step(): came = lax.ppermute(by_h, 'pp', back_again)  34.1 us
    dynamic_slice x22, local copies, waits for them, and re-layouts, step(): was = lax.dynamic_index_in_dim(kept, number, 0, keepdims=False)  33.3 us
  transfers between devices with their start and end apart: 44, of which 30 were waited for; matrix products, arithmetic and copies ran while one was open for 16% of the time, Pallas kernels for 0%

commit v1 on v0

v1 whole, which is shorter than its diff:
```python
import functools

import jax
import jax.numpy as jnp
from jax import lax
from jax.experimental import pallas as pl
from jax.experimental.pallas import tpu as pltpu
from jax.sharding import PartitionSpec as P

C = 2
NH = 8
NG = 4
ND = 2
TN = 512
EPS = 1e-6


def dot(a, b):
    return jnp.dot(a, b, preferred_element_type=jnp.float32)


def kernel(stages, x_hbm, dy_hbm, wg_hbm, wu_hbm, wd_hbm, og_hbm, ou_hbm, od_hbm, spill, wg, wu, wd, wgt, wut, wdt, tg, tu, td, hbuf, gbuf, fsend,
           bsend, keep, back, a_v, act_v, sg, su, sa, at, dt, wsem, xsem, ysem, frecv, fsent, brecv, bsent, keepsem, backsem, fcred, bcred):
    micro, _, rows, d = x_hbm.shape
    ff = wg.shape[1]
    me = lax.axis_index("pp")
    first, last = me == 0, me == stages - 1
    warm = jnp.minimum(stages - me, NH - 1)

    loads = [pltpu.make_async_copy(src.at[0], dst, wsem.at[i]) for i, (src, dst) in enumerate(((wg_hbm, wg), (wu_hbm, wu), (wd_hbm, wd)))]
    for load in loads:
        load.start()

    def x_copy(m):
        return pltpu.make_async_copy(x_hbm.at[m], hbuf.at[lax.rem(m, NH)], xsem)

    def dy_copy(m):
        return pltpu.make_async_copy(dy_hbm.at[m], gbuf.at[lax.rem(m, NG)], ysem)

    @pl.when(first)
    def _():
        x_copy(0).start()

    @pl.when(last)
    def _():
        dy_copy(0).start()

    barrier = pltpu.get_barrier_semaphore()

    @pl.when(me > 0)
    def _():
        pl.semaphore_signal(barrier, inc=1, device_id={"pp": me - 1})

    @pl.when(me < stages - 1)
    def _():
        pl.semaphore_signal(barrier, inc=1, device_id={"pp": me + 1})

    pl.semaphore_wait(barrier, jnp.where(first | last, 1, 2))

    def f_copy(m, c):
        out, slot = lax.rem(m, 2) * C + c, lax.rem(m, NH)
        return pltpu.make_async_remote_copy(
            src_ref=fsend.at[out], dst_ref=hbuf.at[slot, c], send_sem=fsent.at[out], recv_sem=frecv.at[slot * C + c], device_id={"pp": me + 1}
        )

    def b_copy(m, c):
        out, slot = lax.rem(m, 2) * C + c, lax.rem(m, NG)
        return pltpu.make_async_remote_copy(
            src_ref=bsend.at[out], dst_ref=gbuf.at[slot, c], send_sem=bsent.at[out], recv_sem=brecv.at[slot * C + c], device_id={"pp": me - 1}
        )

    def keep_copy(m, c):
        return pltpu.make_async_copy(keep.at[c], spill.at[m, c], keepsem.at[c])

    def back_copy(m, c):
        return pltpu.make_async_copy(spill.at[m, c], back.at[c], backsem.at[c])

    def norm(h):
        wide = h.astype(jnp.float32)
        scale = lax.rsqrt(jnp.mean(wide * wide, -1, keepdims=True) + EPS)
        return wide, scale

    def tiles(body, width=TN, total=ff):
        def one(n, _):
            body(pl.ds(pl.multiple_of(n * width, width), width))
            return 0

        lax.fori_loop(0, total // width, one, 0)

    for load in loads:
        load.wait()

    def forward(m):
        slot = lax.rem(m, NH)

        @pl.when(first)
        def _():
            x_copy(m).wait()

            @pl.when(m + 1 < micro)
            def _():
                x_copy(m + 1).start()

        @pl.when(jnp.logical_not(last) & (m >= NH))
        def _():
            pl.semaphore_wait(fcred, 1)

        def chunk(c, _):
            @pl.when(me > 0)
            def _():
                f_copy(m, c).wait_recv()

            wide, scale = norm(hbuf[slot, c])
            a_v[...] = (wide * scale).astype(jnp.bfloat16)

            def tile(n):
                gate = dot(a_v[...], wg[:, n])
                keep[c, 0, :, n] = gate
                up = dot(a_v[...], wu[:, n])
                keep[c, 1, :, n] = up
                act_v[:, n] = ((gate * jax.nn.sigmoid(gate)) * up).astype(jnp.bfloat16)

            tiles(tile)
            keep_copy(m, c).start()

            @pl.when(me < stages - 1)
            def _():
                @pl.when(m >= 2)
                def _():
                    f_copy(m - 2, c).wait_send()

                out = lax.rem(m, 2) * C + c
                fsend[out] = hbuf[slot, c] + dot(act_v[...], wd[...]).astype(jnp.bfloat16)
                f_copy(m, c).start()

            return 0

        lax.fori_loop(0, C, chunk, 0)

    def backward(m):
        slot, hslot, q = lax.rem(m, NG), lax.rem(m, NH), lax.rem(m, ND)

        @pl.when(last)
        def _():
            dy_copy(m).wait()

            @pl.when(m + 1 < micro)
            def _():
                dy_copy(m + 1).start()

        @pl.when((me > 0) & (m >= NG))
        def _():
            pl.semaphore_wait(bcred, 1)

        def chunk(c, _):
            r = pl.ds(pl.multiple_of(c * rows, rows), rows)

            @pl.when(me < stages - 1)
            def _():
                b_copy(m, c).wait_recv()

            back_copy(m, c).wait()

            def tile(n):
                by_act = dot(gbuf[slot, c], wdt[:, n]).astype(jnp.bfloat16).astype(jnp.float32)
                gate, up = back[c, 0, :, n], back[c, 1, :, n]
                s = jax.nn.sigmoid(gate)
                silu = gate * s
                sa[q, r, n] = (silu * up).astype(jnp.bfloat16)
                su[q, r, n] = (by_act * silu).astype(jnp.bfloat16)
                sg[q, r, n] = ((by_act * up) * (s + silu * (1.0 - s))).astype(jnp.bfloat16)

            tiles(tile)
            wide, scale = norm(hbuf[hslot, c])
            at[q, :, r] = (wide * scale).astype(jnp.bfloat16).T
            dt[q, :, r] = gbuf[slot, c].T

            @pl.when(me > 0)
            def _():
                @pl.when(m >= 2)
                def _():
                    b_copy(m - 2, c).wait_send()

                by_a = dot(sg[q, r, :], wgt[...]).astype(jnp.bfloat16) + dot(su[q, r, :], wut[...]).astype(jnp.bfloat16)
                by_a = by_a.astype(jnp.float32)
                wide, scale = norm(hbuf[hslot, c])
                by_scale = jnp.sum(by_a * wide, -1, keepdims=True)
                by_wide = by_a * scale - wide * (by_scale * (scale * scale * scale) * (1.0 / d))
                bsend[lax.rem(m, 2) * C + c] = by_wide.astype(jnp.bfloat16) + gbuf[slot, c]
                b_copy(m, c).start()

            return 0

        lax.fori_loop(0, C, chunk, 0)

        @pl.when((me > 0) & (m + NH < micro))
        def _():
            pl.semaphore_signal(fcred, inc=1, device_id={"pp": me - 1})

        @pl.when((me < stages - 1) & (m + NG < micro))
        def _():
            pl.semaphore_signal(bcred, inc=1, device_id={"pp": me + 1})

    def term(total, left, right):
        def tile(n):
            total[:, n] += dot(left, right[:, n]).astype(jnp.bfloat16).astype(jnp.float32)

        tiles(tile)

    def step(t, _):
        f, b = t, t - warm
        w = b - (ND - 1)
        q = lax.rem(w + ND * micro, ND)
        f_on, w_on = f < micro, (w >= 0) & (w < micro)

        @pl.when((b >= 0) & (b < micro))
        def _():
            backward(b)

        @pl.when(f_on)
        def _():
            forward(f)

        @pl.when(w_on)
        def _():
            term(tg, at[q], sg.at[q])

        @pl.when(f_on)
        def _():
            for c in range(C):
                keep_copy(f, c).wait()

        @pl.when((b + 1 >= 0) & (b + 1 < micro))
        def _():
            for c in range(C):
                back_copy(b + 1, c).start()

        @pl.when(w_on)
        def _():
            term(tu, at[q], su.at[q])
            term(td, dt[q], sa.at[q])

        return 0

    wgt[...] = wg[...].T
    wut[...] = wu[...].T
    wdt[...] = wd[...].T
    for total in (tg, tu, td):
        total[...] = jnp.zeros_like(total)

    lax.fori_loop(0, micro + NH - 1 + ND - 1, step, 0)

    for m in (micro - 2, micro - 1):
        for c in range(C):
            @pl.when(me < stages - 1)
            def _():
                f_copy(m, c).wait_send()

            @pl.when(me > 0)
            def _():
                b_copy(m, c).wait_send()

    wg[...] = tg[...].astype(jnp.bfloat16)
    wu[...] = tu[...].astype(jnp.bfloat16)
    wd[...] = td[...].astype(jnp.bfloat16).T
    stores = [pltpu.make_async_copy(src, dst.at[0], wsem.at[i]) for i, (src, dst) in enumerate(((wg, og_hbm), (wu, ou_hbm), (wd, od_hbm)))]
    for store in stores:
        store.start()
    for store in stores:
        store.wait()


def solution(mesh):
    stages = mesh.shape["pp"]

    def step(x, dy, w_gate, w_up, w_down):
        micro, tokens, d = x.shape
        ff = w_gate.shape[2]
        rows = tokens // C
        bf16, f32 = jnp.bfloat16, jnp.float32
        anywhere = pl.BlockSpec(memory_space=pl.ANY)
        dma = pltpu.SemaphoreType.DMA
        outs = pl.pallas_call(
            functools.partial(kernel, stages),
            out_shape=(
                jax.ShapeDtypeStruct(w_gate.shape, bf16),
                jax.ShapeDtypeStruct(w_up.shape, bf16),
                jax.ShapeDtypeStruct(w_down.shape, bf16),
                jax.ShapeDtypeStruct((micro, C, 2, rows, ff), f32),
            ),
            in_specs=[anywhere] * 5,
            out_specs=(anywhere,) * 4,
            scratch_shapes=[
                pltpu.VMEM((d, ff), bf16),
                pltpu.VMEM((d, ff), bf16),
                pltpu.VMEM((ff, d), bf16),
                pltpu.VMEM((ff, d), bf16),
                pltpu.VMEM((ff, d), bf16),
                pltpu.VMEM((d, ff), bf16),
                pltpu.VMEM((d, ff), f32),
                pltpu.VMEM((d, ff), f32),
                pltpu.VMEM((d, ff), f32),
                pltpu.VMEM((NH, C, rows, d), bf16),
                pltpu.VMEM((NG, C, rows, d), bf16),
                pltpu.VMEM((2 * C, rows, d), bf16),
                pltpu.VMEM((2 * C, rows, d), bf16),
                pltpu.VMEM((C, 2, rows, ff), f32),
                pltpu.VMEM((C, 2, rows, ff), f32),
                pltpu.VMEM((rows, d), bf16),
                pltpu.VMEM((rows, ff), bf16),
                pltpu.VMEM((ND, tokens, ff), bf16),
                pltpu.VMEM((ND, tokens, ff), bf16),
                pltpu.VMEM((ND, tokens, ff), bf16),
                pltpu.VMEM((ND, d, tokens), bf16),
                pltpu.VMEM((ND, d, tokens), bf16),
                dma((3,)),
                dma,
                dma,
                dma((NH * C,)),
                dma((2 * C,)),
                dma((NG * C,)),
                dma((2 * C,)),
                dma((C,)),
                dma((C,)),
                pltpu.SemaphoreType.REGULAR,
                pltpu.SemaphoreType.REGULAR,
            ],
            compiler_params=pltpu.CompilerParams(collective_id=0, has_side_effects=True, vmem_limit_bytes=67043328),
        )(x.reshape(micro, C, rows, d), dy.reshape(micro, C, rows, d), w_gate, w_up, w_down)
        return outs[:3]

    return jax.shard_map(
        step,
        mesh=mesh,
        in_specs=(P("rep", None, None),) * 2 + (P("pp", None, None),) * 3,
        out_specs=(P(("rep", "pp"), None, None),) * 3,
        check_vma=False,
    )
```

time: 1240 us -> 422 us (0.34); the launches traced: 1220 us -> 422 us
  matrix products: 714 us -> 0 us
  Pallas kernels: 0 us -> 414 us
  starting transfers between devices: 201 us -> 0 us
  waiting for transfers between devices: 164 us -> 0 us
  other arithmetic: 79.6 us -> 0 us
  local copies, waits for them, and re-layouts: 56.6 us -> 6.61 us
    dot_general x226 -> x0, matrix products: 714 us -> none  [the longest x68 276 us: matmul(): jnp.dot(a, w, preferred_element_type=jnp.float32).astype(jnp.bfloat16)]
    pallas_call x0 -> x1, Pallas kernels: none -> 414 us  [step(): pl.pallas_call(functools.partial(kernel, stages), out_shape=(jax.ShapeDty...]
    ppermute x44 -> x0, starting transfers between devices: 201 us -> none  [the longest x22 167 us: step(): came = lax.ppermute(stage(weights, h), 'pp', onward)]
    ppermute x44 -> x0, waiting for transfers between devices: 164 us -> none  [the longest x22 148 us: step(): came = lax.ppermute(by_h, 'pp', back_again)]
    dynamic_update_slice x23 -> x0, other arithmetic: 35.6 us -> none  [step(): lax.dynamic_update_index_in_dim(kept, jnp.where(at_work, h, was), number, 0)]
    dynamic_slice x22 -> x0, local copies, waits for them, and re-layouts: 33.3 us -> none  [step(): was = lax.dynamic_index_in_dim(kept, number, 0, keepdims=False)]
    reduce_sum x23 -> x0, other arithmetic: 32.5 us -> none  [normed(): scale = lax.rsqrt(jnp.mean(wide ** 2, -1, keepdims=True) + 1e-06)]
    unnamed x268 -> x7, local copies, waits for them, and re-layouts: 22.2 us -> 6.61 us
  transfers between devices with their start and end apart: 44 -> 0, of which waited for: 30 -> 0; matrix products, arithmetic and copies ran while one was open for 16% -> 0% of each run, Pallas kernels for 0% -> 0%
where the time goes in v1:
time: 422 us
  Pallas kernels  414 us (98%)
  local copies, waits for them, and re-layouts  6.61 us (2%)
    pallas_call x1, Pallas kernels, step(): pl.pallas_call(functools.partial(kernel, stages), out_shape=(jax.ShapeDty...  414 us

profile of v1, /device:TPU:112, one launch (start us, length us, event | category | flops | bytes accessed | tf_op | source)
XLA Modules:
  0.0 421.8 jit_solution(13400404015092127792)
XLA Ops:
  0.6 414.5 %shard_map.76 = (bf16[1,640,1536]{2,1,0:T(8,128)(2,1)}, bf16[1,640,1536]{2,1,0:T(8,128)(2,1)}, bf16[1,1536,640]{2,1,0:T(8,128)(2,1)}, f32[16,2,2,256,1536]{4,3,2,1,0:T(8,128)}) custom-call(bf16[16,2,256,640]{3,2,1,0:T(8,128)(2,1)} %bitcast.2, bf16[16,2,256,640]{3,2,1,0:T(8,128)(2,1)} %bitcast.3, bf16[1,640,1536]{2,1,0:T(8,128)(2,1)} %wg_hbm.1, ...), custom_call_target="tpu_custom_call" | custom-call | tf_op jit(solution)/shard_map/pallas_call | solution.py:283
  415.1 0.0 copy-start.1
  415.1 3.1 copy.11
  418.2 0.0 copy-done.1
  418.2 0.0 copy-start
  418.2 1.3 copy.12
  419.5 1.0 copy-done
  420.5 1.3 copy.13
Async XLA Ops:
  415.1 3.1 copy-start.1
  418.2 2.3 copy-start

commit v2 on v1

v2 whole, which is shorter than its diff:
```python
import functools

import jax
import jax.numpy as jnp
from jax import lax
from jax.experimental import pallas as pl
from jax.experimental.pallas import tpu as pltpu
from jax.sharding import PartitionSpec as P

Q = 4
COARSE, FINE = 2, 4
FINE_F, FINE_B = 4, 4
NH = 12
NG = 4
ND = 2
TF, TB, TD, TW, TR = 256, 512, 256, 512, 64
EPS = 1e-6


def dot(a, b):
    return jnp.dot(a, b, preferred_element_type=jnp.float32)


def norm(h):
    wide = h.astype(jnp.float32)
    scale = lax.rsqrt(jnp.mean(wide * wide, -1, keepdims=True) + EPS)
    return wide, scale


def kernel(stages, x_hbm, dy_hbm, wg_hbm, wu_hbm, wd_hbm, og_hbm, ou_hbm, od_hbm, spill, acts, wg, wu, wd, wgt, wut, wdt, tg, tu, td, hbuf, gbuf, fsend,
           bsend, keep, back, a_v, act_v, by_a_v, sa, sg, su, at, dt, wsem, xsem, ysem, frecv, fsent, brecv, bsent, keepsem, backsem, fcred, bcred):
    micro, tokens, d = x_hbm.shape
    ff = wg.shape[1]
    part = tokens // Q
    me = lax.axis_index("pp")
    first, last = me == 0, me == stages - 1
    behind = stages - 1 - me
    warm = 1 + lax.div(behind * 4 + 1, 3)
    late = jnp.where(me >= 2, ND - 1, 0)

    loads = [pltpu.make_async_copy(src.at[0], dst, wsem.at[i]) for i, (src, dst) in enumerate(((wg_hbm, wg), (wu_hbm, wu), (wd_hbm, wd)))]
    for load in loads:
        load.start()

    def rows(j, count=1):
        return pl.ds(pl.multiple_of(j * part, part), count * part)

    def x_copy(m):
        return pltpu.make_async_copy(x_hbm.at[m], hbuf.at[lax.rem(m, NH)], xsem)

    def dy_copy(m):
        return pltpu.make_async_copy(dy_hbm.at[m], gbuf.at[lax.rem(m, NG)], ysem)

    @pl.when(first)
    def _():
        x_copy(0).start()

    @pl.when(last)
    def _():
        dy_copy(0).start()

    barrier = pltpu.get_barrier_semaphore()

    @pl.when(me > 0)
    def _():
        pl.semaphore_signal(barrier, inc=1, device_id={"pp": me - 1})

    @pl.when(me < stages - 1)
    def _():
        pl.semaphore_signal(barrier, inc=1, device_id={"pp": me + 1})

    pl.semaphore_wait(barrier, jnp.where(first | last, 1, 2))

    def f_copy(m, j):
        out, slot = lax.rem(m, 2), lax.rem(m, NH)
        return pltpu.make_async_remote_copy(
            src_ref=fsend.at[out, rows(j)], dst_ref=hbuf.at[slot, rows(j)], send_sem=fsent.at[out * Q + j], recv_sem=frecv.at[slot * Q + j],
            device_id={"pp": me + 1},
        )

    def b_copy(m, j):
        out, slot = lax.rem(m, 2), lax.rem(m, NG)
        return pltpu.make_async_remote_copy(
            src_ref=bsend.at[out, rows(j)], dst_ref=gbuf.at[slot, rows(j)], send_sem=bsent.at[out * Q + j], recv_sem=brecv.at[slot * Q + j],
            device_id={"pp": me - 1},
        )

    def keep_copy(m, j):
        return pltpu.make_async_copy(keep.at[:, rows(j)], spill.at[m, :, rows(j)], keepsem.at[j])

    def act_copy(m, j):
        return pltpu.make_async_copy(act_v.at[rows(j)], acts.at[m, rows(j)], keepsem.at[Q + j])

    def back_copy(m, j):
        return pltpu.make_async_copy(spill.at[m, :, rows(j)], back.at[:, rows(j)], backsem.at[j])

    def sa_copy(m):
        return pltpu.make_async_copy(acts.at[m], sa, backsem.at[Q])

    for load in loads:
        load.wait()

    def forward(m, blocks):
        slot, out, each = lax.rem(m, NH), lax.rem(m, 2), Q // blocks

        def hidden(r):
            wide, scale = norm(hbuf[slot, r])
            a = (wide * scale).astype(jnp.bfloat16)
            a_v[r, :] = a
            for n in range(0, ff, TF):
                n = slice(n, n + TF)
                gate, up = dot(a_v[r, :], wg[:, n]), dot(a_v[r, :], wu[:, n])
                s = jax.nn.sigmoid(gate)
                silu = gate * s
                keep[0, r, n] = silu
                keep[1, r, n] = up * (s + silu * (1.0 - s))
                act_v[r, n] = (silu * up).astype(jnp.bfloat16)

        def block(i, _):
            r = rows(i * each, each)
            for j in range(each):
                @pl.when(me > 0)
                def _():
                    f_copy(m, i * each + j).wait_recv()

                @pl.when((me < stages - 1) & (m >= 2))
                def _():
                    f_copy(m - 2, i * each + j).wait_send()

            @pl.when(last)
            def _():
                hidden(r)

            @pl.when(me < stages - 1)
            def _():
                hidden(r)
                for n in range(0, d, TD):
                    n = slice(n, min(n + TD, d))
                    fsend[out, r, n] = hbuf[slot, r, n] + dot(act_v[r, :], wd[:, n]).astype(jnp.bfloat16)
                for j in range(each):
                    f_copy(m, i * each + j).start()

            for j in range(each):
                keep_copy(m, i * each + j).start()
                act_copy(m, i * each + j).start()

            return 0

        lax.fori_loop(0, blocks, block, 0)

    def forwards(m):
        @pl.when(first)
        def _():
            x_copy(m).wait()

            @pl.when(m + 1 < micro)
            def _():
                x_copy(m + 1).start()

        @pl.when((me < stages - 1) & (m >= NH))
        def _():
            pl.semaphore_wait(fcred, 1)

        @pl.when(m < FINE_F)
        def _():
            forward(m, FINE)

        @pl.when(m >= FINE_F)
        def _():
            forward(m, COARSE)

    def backward(m, blocks):
        slot, hslot, q, out, each = lax.rem(m, NG), lax.rem(m, NH), lax.rem(m, ND), lax.rem(m, 2), Q // blocks

        def hidden(r):
            for n in range(0, ff, TB):
                n = slice(n, n + TB)
                by_act = dot(gbuf[slot, r], wdt[:, n]).astype(jnp.bfloat16).astype(jnp.float32)
                su[q, r, n] = (by_act * back[0, r, n]).astype(jnp.bfloat16)
                sg[q, r, n] = (by_act * back[1, r, n]).astype(jnp.bfloat16)
            wide, scale = norm(hbuf[hslot, r])
            at[q, :, r] = (wide * scale).astype(jnp.bfloat16).T
            dt[q, :, r] = gbuf[slot, r].T

        def block(i, _):
            r = rows(i * each, each)
            for j in range(each):
                @pl.when(me < stages - 1)
                def _():
                    b_copy(m, i * each + j).wait_recv()

                @pl.when((me > 0) & (m >= 2))
                def _():
                    b_copy(m - 2, i * each + j).wait_send()

                back_copy(m, i * each + j).wait()

            @pl.when(first)
            def _():
                hidden(r)

            @pl.when(me > 0)
            def _():
                hidden(r)
                for n in range(0, d, TD):
                    n = slice(n, min(n + TD, d))
                    by_a_v[0 : each * part, n] = dot(sg[q, r, :], wgt[:, n]).astype(jnp.bfloat16) + dot(su[q, r, :], wut[:, n]).astype(jnp.bfloat16)
                for p in range(0, each * part, TR):
                    o = pl.ds(pl.multiple_of(i * each * part + p, TR), TR)
                    by_a = by_a_v[p : p + TR, :].astype(jnp.float32)
                    wide, scale = norm(hbuf[hslot, o])
                    by_scale = jnp.sum(by_a * wide, -1, keepdims=True)
                    by_wide = by_a * scale - wide * (by_scale * (scale * scale * scale) * (1.0 / d))
                    bsend[out, o] = by_wide.astype(jnp.bfloat16) + gbuf[slot, o]
                for j in range(each):
                    b_copy(m, i * each + j).start()

            return 0

        lax.fori_loop(0, blocks, block, 0)

    def backwards(m):
        @pl.when(last)
        def _():
            dy_copy(m).wait()

            @pl.when(m + 1 < micro)
            def _():
                dy_copy(m + 1).start()

        @pl.when((me > 0) & (m >= NG))
        def _():
            pl.semaphore_wait(bcred, 1)

        @pl.when(m < micro - FINE_B)
        def _():
            backward(m, COARSE)

        @pl.when(m >= micro - FINE_B)
        def _():
            backward(m, FINE)

        @pl.when((me > 0) & (m + NH < micro))
        def _():
            pl.semaphore_signal(fcred, inc=1, device_id={"pp": me - 1})

        @pl.when((me < stages - 1) & (m + NG < micro))
        def _():
            pl.semaphore_signal(bcred, inc=1, device_id={"pp": me + 1})

    def term(total, left, right):
        for n in range(0, ff, TW):
            n = slice(n, n + TW)
            total[:, n] += dot(left[...], right[:, n]).astype(jnp.bfloat16).astype(jnp.float32)

    def step(t, _):
        f, b = t, t - warm
        w = b - late
        q = lax.rem(w + ND * micro, ND)
        f_on, w_on, more = f < micro, (w >= 0) & (w < micro), (b + 1 >= 0) & (b + 1 < micro)

        @pl.when((b >= 0) & (b < micro))
        def _():
            backwards(b)

        @pl.when(more & (warm > 1))
        def _():
            for j in range(Q):
                back_copy(b + 1, j).start()

        @pl.when(f_on)
        def _():
            forwards(f)

        @pl.when(w_on)
        def _():
            term(tg, at.at[q], sg.at[q])

        @pl.when(f_on)
        def _():
            for j in range(Q):
                keep_copy(f, j).wait()
                act_copy(f, j).wait()

        @pl.when(more & (warm == 1))
        def _():
            for j in range(Q):
                back_copy(b + 1, j).start()

        @pl.when(w_on)
        def _():
            term(tu, at.at[q], su.at[q])
            sa_copy(w).wait()
            term(td, dt.at[q], sa)

        @pl.when((w + 1 >= 0) & (w + 1 < micro))
        def _():
            sa_copy(w + 1).start()

        return 0

    wgt[...] = wg[...].T
    wut[...] = wu[...].T
    wdt[...] = wd[...].T
    for total in (tg, tu, td):
        total[...] = jnp.zeros_like(total)

    lax.fori_loop(0, micro + warm + late, step, 0)

    for m in (micro - 2, micro - 1):
        for j in range(Q):
            @pl.when(me < stages - 1)
            def _():
                f_copy(m, j).wait_send()

            @pl.when(me > 0)
            def _():
                b_copy(m, j).wait_send()

    wg[...] = tg[...].astype(jnp.bfloat16)
    wu[...] = tu[...].astype(jnp.bfloat16)
    wd[...] = td[...].astype(jnp.bfloat16).T
    stores = [pltpu.make_async_copy(src, dst.at[0], wsem.at[i]) for i, (src, dst) in enumerate(((wg, og_hbm), (wu, ou_hbm), (wd, od_hbm)))]
    for store in stores:
        store.start()
    for store in stores:
        store.wait()


def solution(mesh):
    stages = mesh.shape["pp"]

    def step(x, dy, w_gate, w_up, w_down):
        micro, tokens, d = x.shape
        ff = w_gate.shape[2]
        bf16, f32 = jnp.bfloat16, jnp.float32
        anywhere = pl.BlockSpec(memory_space=pl.ANY)
        dma = pltpu.SemaphoreType.DMA
        outs = pl.pallas_call(
            functools.partial(kernel, stages),
            out_shape=(
                jax.ShapeDtypeStruct(w_gate.shape, bf16),
                jax.ShapeDtypeStruct(w_up.shape, bf16),
                jax.ShapeDtypeStruct(w_down.shape, bf16),
                jax.ShapeDtypeStruct((micro, 2, tokens, ff), f32),
                jax.ShapeDtypeStruct((micro, tokens, ff), bf16),
            ),
            in_specs=[anywhere] * 5,
            out_specs=(anywhere,) * 5,
            scratch_shapes=[
                pltpu.VMEM((d, ff), bf16),
                pltpu.VMEM((d, ff), bf16),
                pltpu.VMEM((ff, d), bf16),
                pltpu.VMEM((ff, d), bf16),
                pltpu.VMEM((ff, d), bf16),
                pltpu.VMEM((d, ff), bf16),
                pltpu.VMEM((d, ff), f32),
                pltpu.VMEM((d, ff), f32),
                pltpu.VMEM((d, ff), f32),
                pltpu.VMEM((NH, tokens, d), bf16),
                pltpu.VMEM((NG, tokens, d), bf16),
                pltpu.VMEM((2, tokens, d), bf16),
                pltpu.VMEM((2, tokens, d), bf16),
                pltpu.VMEM((2, tokens, ff), f32),
                pltpu.VMEM((2, tokens, ff), f32),
                pltpu.VMEM((tokens, d), bf16),
                pltpu.VMEM((tokens, ff), bf16),
                pltpu.VMEM((tokens // COARSE, d), bf16),
                pltpu.VMEM((tokens, ff), bf16),
                pltpu.VMEM((ND, tokens, ff), bf16),
                pltpu.VMEM((ND, tokens, ff), bf16),
                pltpu.VMEM((ND, d, tokens), bf16),
                pltpu.VMEM((ND, d, tokens), bf16),
                dma((3,)),
                dma,
                dma,
                dma((NH * Q,)),
                dma((2 * Q,)),
                dma((NG * Q,)),
                dma((2 * Q,)),
                dma((2 * Q,)),
                dma((Q + 1,)),
                pltpu.SemaphoreType.REGULAR,
                pltpu.SemaphoreType.REGULAR,
            ],
            compiler_params=pltpu.CompilerParams(collective_id=0, has_side_effects=True, vmem_limit_bytes=67043328),
        )(x, dy, w_gate, w_up, w_down)
        return outs[:3]

    return jax.shard_map(
        step,
        mesh=mesh,
        in_specs=(P("rep", None, None),) * 2 + (P("pp", None, None),) * 3,
        out_specs=(P(("rep", "pp"), None, None),) * 3,
        check_vma=False,
    )
```

time: 422 us -> 309 us (0.73)
  Pallas kernels: 414 us -> 301 us
    pallas_call x1, Pallas kernels: 414 us -> 301 us  [step(): pl.pallas_call(functools.partial(kernel, stages), out_shape=(jax.ShapeDty...]
where the time goes in v2:
time: 309 us
  Pallas kernels  301 us (97%)
  local copies, waits for them, and re-layouts  6.61 us (2%)
    pallas_call x1, Pallas kernels, step(): pl.pallas_call(functools.partial(kernel, stages), out_shape=(jax.ShapeDty...  301 us
    unnamed x7, local copies, waits for them, and re-layouts  6.61 us

profile of v2, /device:TPU:112, one launch (start us, length us, event | category | flops | bytes accessed | tf_op | source)
XLA Modules:
  0.0 308.6 jit_solution(9313858899300235244)
XLA Ops:
  0.6 301.3 %shard_map.76 = (bf16[1,640,1536]{2,1,0:T(8,128)(2,1)}, bf16[1,640,1536]{2,1,0:T(8,128)(2,1)}, bf16[1,1536,640]{2,1,0:T(8,128)(2,1)}, f32[16,2,512,1536]{3,2,1,0:T(8,128)}, bf16[16,512,1536]{2,1,0:T(8,128)(2,1)}) custom-call(bf16[16,512,640]{2,1,0:T(8,128)(2,1)} %x_hbm.1, bf16[16,512,640]{2,1,0:T(8,128)(2,1)} %dy_hbm.1, bf16[1,640,1536]{2,1,0:T(8,128)(2,1)} %wg_hbm.1, ...), custom_call_target="tpu_custom_call" | custom-call | tf_op jit(solution)/shard_map/pallas_call | solution.py:339
  301.9 0.0 copy-start.1
  301.9 3.1 copy.11
  305.0 0.0 copy-done.1
  305.0 0.0 copy-start
  305.0 1.3 copy.12
  306.3 1.0 copy-done
  307.3 1.3 copy.13
Async XLA Ops:
  301.9 3.1 %copy-start.1 = (bf16[1,640,1536]{2,1,0:T(8,128)(2,1)S(1)}, bf16[1,640,1536]{2,1,0:T(8,128)(2,1)}, u32[]{:S(2)}) copy-start(bf16[1,640,1536]{2,1,0:T(8,128)(2,1)} %get-tuple-element.13) | copy-start | bytes 5898244
  305.0 2.3 copy-start

commit v3 on v2

--- a/solution.py
+++ b/solution.py
@@ -9,9 +9,9 @@
 
 Q = 4
 COARSE, FINE = 2, 4
-FINE_F, FINE_B = 4, 4
-NH = 12
-NG = 4
+FINE_F, FINE_B = 5, 5
+NH = 14
+NG = 3
 ND = 2
 TF, TB, TD, TW, TR = 256, 512, 256, 512, 64
 EPS = 1e-6
@@ -19,6 +19,10 @@
 
 def dot(a, b):
     return jnp.dot(a, b, preferred_element_type=jnp.float32)
+
+
+def dot_t(a, b):
+    return lax.dot_general(a, b, (((1,), (1,)), ((), ())), preferred_element_type=jnp.float32)
 
 
 def norm(h):
@@ -35,8 +39,8 @@
     me = lax.axis_index("pp")
     first, last = me == 0, me == stages - 1
     behind = stages - 1 - me
-    warm = 1 + lax.div(behind * 4 + 1, 3)
-    late = jnp.where(me >= 2, ND - 1, 0)
+    warm = jnp.minimum(1 + lax.div(behind * 3, 2) + jnp.where(me < 2, 4, 0), NH - 1)
+    late = jnp.clip(me - 2, 0, ND - 1)
 
     loads = [pltpu.make_async_copy(src.at[0], dst, wsem.at[i]) for i, (src, dst) in enumerate(((wg_hbm, wg), (wu_hbm, wu), (wd_hbm, wd)))]
     for load in loads:
@@ -134,9 +138,12 @@
             @pl.when(me < stages - 1)
             def _():
                 hidden(r)
-                for n in range(0, d, TD):
-                    n = slice(n, min(n + TD, d))
-                    fsend[out, r, n] = hbuf[slot, r, n] + dot(act_v[r, :], wd[:, n]).astype(jnp.bfloat16)
+                if blocks == COARSE:
+                    fsend[out, r] = hbuf[slot, r] + dot_t(wdt[...], act_v[r, :]).astype(jnp.bfloat16).T
+                else:
+                    for n in range(0, d, TD):
+                        n = slice(n, min(n + TD, d))
+                        fsend[out, r, n] = hbuf[slot, r, n] + dot(act_v[r, :], wd[:, n]).astype(jnp.bfloat16)
                 for j in range(each):
                     f_copy(m, i * each + j).start()
 
@@ -202,9 +209,14 @@
             @pl.when(me > 0)
             def _():
                 hidden(r)
-                for n in range(0, d, TD):
-                    n = slice(n, min(n + TD, d))
-                    by_a_v[0 : each * part, n] = dot(sg[q, r, :], wgt[:, n]).astype(jnp.bfloat16) + dot(su[q, r, :], wut[:, n]).astype(jnp.bfloat16)
+                if blocks == COARSE:
+                    by_at = dot_t(wg[...], sg[q, r, :]).astype(jnp.bfloat16) + dot_t(wu[...], su[q, r, :]).astype(jnp.bfloat16)
+                    by_a_v[...] = by_at.T
+                else:
+                    for n in range(0, d, TD):
+                        n = slice(n, min(n + TD, d))
+                        by_a = dot(sg[q, r, :], wgt[:, n]).astype(jnp.bfloat16) + dot(su[q, r, :], wut[:, n]).astype(jnp.bfloat16)
+                        by_a_v[0 : each * part, n] = by_a
                 for p in range(0, each * part, TR):
                     o = pl.ds(pl.multiple_of(i * each * part + p, TR), TR)
                     by_a = by_a_v[p : p + TR, :].astype(jnp.float32)
@@ -272,11 +284,19 @@
         def _():
             forwards(f)
 
+        @pl.when(t == 0)
+        def _():
+            for total in (tg, tu, td):
+                total[...] = jnp.zeros_like(total)
+            wgt[...] = wg[...].T
+            wut[...] = wu[...].T
+            wdt[...] = wd[...].T
+
         @pl.when(w_on)
         def _():
             term(tg, at.at[q], sg.at[q])
 
-        @pl.when(f_on)
+        @pl.when(f_on & (warm == 1))
         def _():
             for j in range(Q):
                 keep_copy(f, j).wait()
@@ -293,17 +313,17 @@
             sa_copy(w).wait()
             term(td, dt.at[q], sa)
 
+        @pl.when(f_on & (warm > 1))
+        def _():
+            for j in range(Q):
+                keep_copy(f, j).wait()
+                act_copy(f, j).wait()
+
         @pl.when((w + 1 >= 0) & (w + 1 < micro))
         def _():
             sa_copy(w + 1).start()
 
         return 0
-
-    wgt[...] = wg[...].T
-    wut[...] = wu[...].T
-    wdt[...] = wd[...].T
-    for total in (tg, tu, td):
-        total[...] = jnp.zeros_like(total)
 
     lax.fori_loop(0, micro + warm + late, step, 0)
 
@@ -317,12 +337,13 @@
             def _():
                 b_copy(m, j).wait_send()
 
+    stores = [pltpu.make_async_copy(src, dst.at[0], wsem.at[i]) for i, (src, dst) in enumerate(((wg, og_hbm), (wu, ou_hbm), (wd, od_hbm)))]
     wg[...] = tg[...].astype(jnp.bfloat16)
+    stores[0].start()
     wu[...] = tu[...].astype(jnp.bfloat16)
+    stores[1].start()
     wd[...] = td[...].astype(jnp.bfloat16).T
-    stores = [pltpu.make_async_copy(src, dst.at[0], wsem.at[i]) for i, (src, dst) in enumerate(((wg, og_hbm), (wu, ou_hbm), (wd, od_hbm)))]
-    for store in stores:
-        store.start()
+    stores[2].start()
     for store in stores:
         store.wait()
 

time: 309 us -> 267 us (0.86)
  Pallas kernels: 301 us -> 260 us
    pallas_call x1, Pallas kernels: 301 us -> 260 us  [step(): pl.pallas_call(functools.partial(kernel, stages), out_shape=(jax.ShapeDty...]
where the time goes in v3:
time: 267 us
  Pallas kernels  260 us (97%)
  local copies, waits for them, and re-layouts  6.61 us (2%)
    pallas_call x1, Pallas kernels, step(): pl.pallas_call(functools.partial(kernel, stages), out_shape=(jax.ShapeDty...  260 us
    unnamed x7, local copies, waits for them, and re-layouts  6.61 us

profile of v3, /device:TPU:112, one launch (start us, length us, event | category | flops | bytes accessed | tf_op | source)
XLA Modules:
  0.0 267.2 jit_solution(5748142070916809077)
XLA Ops:
  0.6 259.9 %shard_map.76 = (bf16[1,640,1536]{2,1,0:T(8,128)(2,1)}, bf16[1,640,1536]{2,1,0:T(8,128)(2,1)}, bf16[1,1536,640]{2,1,0:T(8,128)(2,1)}, f32[16,2,512,1536]{3,2,1,0:T(8,128)}, bf16[16,512,1536]{2,1,0:T(8,128)(2,1)}) custom-call(bf16[16,512,640]{2,1,0:T(8,128)(2,1)} %x_hbm.1, bf16[16,512,640]{2,1,0:T(8,128)(2,1)} %dy_hbm.1, bf16[1,640,1536]{2,1,0:T(8,128)(2,1)} %wg_hbm.1, ...), custom_call_target="tpu_custom_call" | custom-call | tf_op jit(solution)/shard_map/pallas_call | solution.py:360
  260.6 0.0 copy-start.1
  260.6 3.1 %copy.11 = bf16[1,640,1536]{2,1,0:T(8,128)(2,1)} copy(bf16[1,640,1536]{2,1,0:T(8,128)(2,1)} %get-tuple-element.12) | data formatting | bytes 3932160
  263.7 0.0 copy-done.1
  263.7 0.0 copy-start
  263.7 1.3 copy.12
  264.9 1.0 copy-done
  265.9 1.3 copy.13
Async XLA Ops:
  260.6 3.1 %copy-start.1 = (bf16[1,640,1536]{2,1,0:T(8,128)(2,1)S(1)}, bf16[1,640,1536]{2,1,0:T(8,128)(2,1)}, u32[]{:S(2)}) copy-start(bf16[1,640,1536]{2,1,0:T(8,128)(2,1)} %get-tuple-element.13) | copy-start | bytes 5898244
  263.7 2.3 copy-start

commit v4 on v3

--- a/solution.py
+++ b/solution.py
@@ -32,7 +32,7 @@
 
 
 def kernel(stages, x_hbm, dy_hbm, wg_hbm, wu_hbm, wd_hbm, og_hbm, ou_hbm, od_hbm, spill, acts, wg, wu, wd, wgt, wut, wdt, tg, tu, td, hbuf, gbuf, fsend,
-           bsend, keep, back, a_v, act_v, by_a_v, sa, sg, su, at, dt, wsem, xsem, ysem, frecv, fsent, brecv, bsent, keepsem, backsem, fcred, bcred):
+           bsend, pool, a_v, act_v, by_a_v, sa, sg, su, at, dt, wsem, xsem, ysem, frecv, fsent, brecv, bsent, keepsem, backsem, fcred, bcred):
     micro, tokens, d = x_hbm.shape
     ff = wg.shape[1]
     part = tokens // Q
@@ -41,6 +41,7 @@
     behind = stages - 1 - me
     warm = jnp.minimum(1 + lax.div(behind * 3, 2) + jnp.where(me < 2, 4, 0), NH - 1)
     late = jnp.clip(me - 2, 0, ND - 1)
+    resident = warm <= 2
 
     loads = [pltpu.make_async_copy(src.at[0], dst, wsem.at[i]) for i, (src, dst) in enumerate(((wg_hbm, wg), (wu_hbm, wu), (wd_hbm, wd)))]
     for load in loads:
@@ -90,13 +91,13 @@
         )
 
     def keep_copy(m, j):
-        return pltpu.make_async_copy(keep.at[:, rows(j)], spill.at[m, :, rows(j)], keepsem.at[j])
+        return pltpu.make_async_copy(pool.at[0, :, rows(j)], spill.at[m, :, rows(j)], keepsem.at[j])
 
     def act_copy(m, j):
         return pltpu.make_async_copy(act_v.at[rows(j)], acts.at[m, rows(j)], keepsem.at[Q + j])
 
     def back_copy(m, j):
-        return pltpu.make_async_copy(spill.at[m, :, rows(j)], back.at[:, rows(j)], backsem.at[j])
+        return pltpu.make_async_copy(spill.at[m, :, rows(j)], pool.at[1, :, rows(j)], backsem.at[j])
 
     def sa_copy(m):
         return pltpu.make_async_copy(acts.at[m], sa, backsem.at[Q])
@@ -106,6 +107,7 @@
 
     def forward(m, blocks):
         slot, out, each = lax.rem(m, NH), lax.rem(m, 2), Q // blocks
+        place = jnp.where(resident, lax.rem(m, 2), 0)
 
         def hidden(r):
             wide, scale = norm(hbuf[slot, r])
@@ -116,8 +118,8 @@
                 gate, up = dot(a_v[r, :], wg[:, n]), dot(a_v[r, :], wu[:, n])
                 s = jax.nn.sigmoid(gate)
                 silu = gate * s
-                keep[0, r, n] = silu
-                keep[1, r, n] = up * (s + silu * (1.0 - s))
+                pool[place, 0, r, n] = silu
+                pool[place, 1, r, n] = up * (s + silu * (1.0 - s))
                 act_v[r, n] = (silu * up).astype(jnp.bfloat16)
 
         def block(i, _):
@@ -148,8 +150,11 @@
                     f_copy(m, i * each + j).start()
 
             for j in range(each):
-                keep_copy(m, i * each + j).start()
                 act_copy(m, i * each + j).start()
+
+                @pl.when(jnp.logical_not(resident))
+                def _():
+                    keep_copy(m, i * each + j).start()
 
             return 0
 
@@ -178,13 +183,14 @@
 
     def backward(m, blocks):
         slot, hslot, q, out, each = lax.rem(m, NG), lax.rem(m, NH), lax.rem(m, ND), lax.rem(m, 2), Q // blocks
+        place = jnp.where(resident, lax.rem(m, 2), 1)
 
         def hidden(r):
             for n in range(0, ff, TB):
                 n = slice(n, n + TB)
                 by_act = dot(gbuf[slot, r], wdt[:, n]).astype(jnp.bfloat16).astype(jnp.float32)
-                su[q, r, n] = (by_act * back[0, r, n]).astype(jnp.bfloat16)
-                sg[q, r, n] = (by_act * back[1, r, n]).astype(jnp.bfloat16)
+                su[q, r, n] = (by_act * pool[place, 0, r, n]).astype(jnp.bfloat16)
+                sg[q, r, n] = (by_act * pool[place, 1, r, n]).astype(jnp.bfloat16)
             wide, scale = norm(hbuf[hslot, r])
             at[q, :, r] = (wide * scale).astype(jnp.bfloat16).T
             dt[q, :, r] = gbuf[slot, r].T
@@ -200,7 +206,9 @@
                 def _():
                     b_copy(m - 2, i * each + j).wait_send()
 
-                back_copy(m, i * each + j).wait()
+                @pl.when(jnp.logical_not(resident))
+                def _():
+                    back_copy(m, i * each + j).wait()
 
             @pl.when(first)
             def _():
@@ -265,6 +273,8 @@
             n = slice(n, n + TW)
             total[:, n] += dot(left[...], right[:, n]).astype(jnp.bfloat16).astype(jnp.float32)
 
+    stores = [pltpu.make_async_copy(src, dst.at[0], wsem.at[i]) for i, (src, dst) in enumerate(((wg, og_hbm), (wu, ou_hbm), (wd, od_hbm)))]
+
     def step(t, _):
         f, b = t, t - warm
         w = b - late
@@ -275,7 +285,7 @@
         def _():
             backwards(b)
 
-        @pl.when(more & (warm > 1))
+        @pl.when(more & jnp.logical_not(resident))
         def _():
             for j in range(Q):
                 back_copy(b + 1, j).start()
@@ -294,30 +304,34 @@
 
         @pl.when(w_on)
         def _():
+            sa_copy(w).wait()
+
+        @pl.when(w_on & (w < micro - 1))
+        def _():
             term(tg, at.at[q], sg.at[q])
-
-        @pl.when(f_on & (warm == 1))
+            term(tu, at.at[q], su.at[q])
+            term(td, dt.at[q], sa)
+
+        @pl.when(w == micro - 1)
+        def _():
+            term(tg, at.at[q], sg.at[q])
+            wg[...] = tg[...].astype(jnp.bfloat16)
+            stores[0].start()
+            term(tu, at.at[q], su.at[q])
+            wu[...] = tu[...].astype(jnp.bfloat16)
+            stores[1].start()
+            term(td, dt.at[q], sa)
+            wd[...] = td[...].astype(jnp.bfloat16).T
+            stores[2].start()
+
+        @pl.when(f_on)
         def _():
             for j in range(Q):
-                keep_copy(f, j).wait()
                 act_copy(f, j).wait()
 
-        @pl.when(more & (warm == 1))
-        def _():
-            for j in range(Q):
-                back_copy(b + 1, j).start()
-
-        @pl.when(w_on)
-        def _():
-            term(tu, at.at[q], su.at[q])
-            sa_copy(w).wait()
-            term(td, dt.at[q], sa)
-
-        @pl.when(f_on & (warm > 1))
-        def _():
-            for j in range(Q):
-                keep_copy(f, j).wait()
-                act_copy(f, j).wait()
+                @pl.when(jnp.logical_not(resident))
+                def _():
+                    keep_copy(f, j).wait()
 
         @pl.when((w + 1 >= 0) & (w + 1 < micro))
         def _():
@@ -337,13 +351,6 @@
             def _():
                 b_copy(m, j).wait_send()
 
-    stores = [pltpu.make_async_copy(src, dst.at[0], wsem.at[i]) for i, (src, dst) in enumerate(((wg, og_hbm), (wu, ou_hbm), (wd, od_hbm)))]
-    wg[...] = tg[...].astype(jnp.bfloat16)
-    stores[0].start()
-    wu[...] = tu[...].astype(jnp.bfloat16)
-    stores[1].start()
-    wd[...] = td[...].astype(jnp.bfloat16).T
-    stores[2].start()
     for store in stores:
         store.wait()
 
@@ -382,8 +389,7 @@
                 pltpu.VMEM((NG, tokens, d), bf16),
                 pltpu.VMEM((2, tokens, d), bf16),
                 pltpu.VMEM((2, tokens, d), bf16),
-                pltpu.VMEM((2, tokens, ff), f32),
-                pltpu.VMEM((2, tokens, ff), f32),
+                pltpu.VMEM((2, 2, tokens, ff), f32),
                 pltpu.VMEM((tokens, d), bf16),
                 pltpu.VMEM((tokens, ff), bf16),
                 pltpu.VMEM((tokens // COARSE, d), bf16),

time: 267 us -> 259 us (0.970)
  Pallas kernels: 260 us -> 252 us
    pallas_call x1, Pallas kernels: 260 us -> 252 us  [step(): pl.pallas_call(functools.partial(kernel, stages), out_shape=(jax.ShapeDty...]
where the time goes in v4:
time: 259 us
  Pallas kernels  252 us (97%)
  local copies, waits for them, and re-layouts  6.61 us (3%)
    pallas_call x1, Pallas kernels, step(): pl.pallas_call(functools.partial(kernel, stages), out_shape=(jax.ShapeDty...  252 us
    unnamed x7, local copies, waits for them, and re-layouts  6.61 us

profile of v4, /device:TPU:112, one launch (start us, length us, event | category | flops | bytes accessed | tf_op | source)
XLA Modules:
  0.0 259.2 jit_solution(11772564411074799918)
XLA Ops:
  0.6 251.9 %shard_map.76 = (bf16[1,640,1536]{2,1,0:T(8,128)(2,1)}, bf16[1,640,1536]{2,1,0:T(8,128)(2,1)}, bf16[1,1536,640]{2,1,0:T(8,128)(2,1)}, f32[16,2,512,1536]{3,2,1,0:T(8,128)}, bf16[16,512,1536]{2,1,0:T(8,128)(2,1)}) custom-call(bf16[16,512,640]{2,1,0:T(8,128)(2,1)} %x_hbm.1, bf16[16,512,640]{2,1,0:T(8,128)(2,1)} %dy_hbm.1, bf16[1,640,1536]{2,1,0:T(8,128)(2,1)} %wg_hbm.1, ...), custom_call_target="tpu_custom_call" | custom-call | tf_op jit(solution)/shard_map/pallas_call | solution.py:367
  252.5 0.0 copy-start.1
  252.5 3.1 %copy.11 = bf16[1,640,1536]{2,1,0:T(8,128)(2,1)} copy(bf16[1,640,1536]{2,1,0:T(8,128)(2,1)} %get-tuple-element.12) | data formatting | bytes 3932160
  255.6 0.0 copy-done.1
  255.6 0.0 copy-start
  255.6 1.3 copy.12
  256.9 1.0 copy-done
  257.9 1.3 copy.13
Async XLA Ops:
  252.5 3.1 %copy-start.1 = (bf16[1,640,1536]{2,1,0:T(8,128)(2,1)S(1)}, bf16[1,640,1536]{2,1,0:T(8,128)(2,1)}, u32[]{:S(2)}) copy-start(bf16[1,640,1536]{2,1,0:T(8,128)(2,1)} %get-tuple-element.13) | copy-start | bytes 5898244
  255.6 2.3 copy-start

commit v5 on v4

--- a/solution.py
+++ b/solution.py
@@ -9,7 +9,7 @@
 
 Q = 4
 COARSE, FINE = 2, 4
-FINE_F, FINE_B = 5, 5
+FINE_F, FINE_B = 5, 4
 NH = 14
 NG = 3
 ND = 2
@@ -40,7 +40,7 @@
     first, last = me == 0, me == stages - 1
     behind = stages - 1 - me
     warm = jnp.minimum(1 + lax.div(behind * 3, 2) + jnp.where(me < 2, 4, 0), NH - 1)
-    late = jnp.clip(me - 2, 0, ND - 1)
+    late = jnp.where((me >= 2) & (me < stages - 1), ND - 1, 0)
     resident = warm <= 2
 
     loads = [pltpu.make_async_copy(src.at[0], dst, wsem.at[i]) for i, (src, dst) in enumerate(((wg_hbm, wg), (wu_hbm, wu), (wd_hbm, wd)))]
@@ -124,13 +124,15 @@
 
         def block(i, _):
             r = rows(i * each, each)
-            for j in range(each):
-                @pl.when(me > 0)
-                def _():
+
+            @pl.when(me > 0)
+            def _():
+                for j in range(each):
                     f_copy(m, i * each + j).wait_recv()
 
-                @pl.when((me < stages - 1) & (m >= 2))
-                def _():
+            @pl.when((me < stages - 1) & (m >= 2))
+            def _():
+                for j in range(each):
                     f_copy(m - 2, i * each + j).wait_send()
 
             @pl.when(last)
@@ -152,8 +154,9 @@
             for j in range(each):
                 act_copy(m, i * each + j).start()
 
-                @pl.when(jnp.logical_not(resident))
-                def _():
+            @pl.when(jnp.logical_not(resident))
+            def _():
+                for j in range(each):
                     keep_copy(m, i * each + j).start()
 
             return 0
@@ -197,17 +200,20 @@
 
         def block(i, _):
             r = rows(i * each, each)
-            for j in range(each):
-                @pl.when(me < stages - 1)
-                def _():
+
+            @pl.when(me < stages - 1)
+            def _():
+                for j in range(each):
                     b_copy(m, i * each + j).wait_recv()
 
-                @pl.when((me > 0) & (m >= 2))
-                def _():
+            @pl.when((me > 0) & (m >= 2))
+            def _():
+                for j in range(each):
                     b_copy(m - 2, i * each + j).wait_send()
 
-                @pl.when(jnp.logical_not(resident))
-                def _():
+            @pl.when(jnp.logical_not(resident))
+            def _():
+                for j in range(each):
                     back_copy(m, i * each + j).wait()
 
             @pl.when(first)
@@ -302,18 +308,16 @@
             wut[...] = wu[...].T
             wdt[...] = wd[...].T
 
-        @pl.when(w_on)
+        @pl.when(w_on & (w < micro - 1))
         def _():
             sa_copy(w).wait()
-
-        @pl.when(w_on & (w < micro - 1))
-        def _():
             term(tg, at.at[q], sg.at[q])
             term(tu, at.at[q], su.at[q])
             term(td, dt.at[q], sa)
 
         @pl.when(w == micro - 1)
         def _():
+            sa_copy(w).wait()
             term(tg, at.at[q], sg.at[q])
             wg[...] = tg[...].astype(jnp.bfloat16)
             stores[0].start()
@@ -329,8 +333,9 @@
             for j in range(Q):
                 act_copy(f, j).wait()
 
-                @pl.when(jnp.logical_not(resident))
-                def _():
+            @pl.when(jnp.logical_not(resident))
+            def _():
+                for j in range(Q):
                     keep_copy(f, j).wait()
 
         @pl.when((w + 1 >= 0) & (w + 1 < micro))

time: 259 us -> 258 us (level)
  no operation moved by 1% of the time
where the time goes in v5:
time: 258 us
  Pallas kernels  251 us (97%)
  local copies, waits for them, and re-layouts  6.61 us (3%)
    pallas_call x1, Pallas kernels, step(): pl.pallas_call(functools.partial(kernel, stages), out_shape=(jax.ShapeDty...  251 us
    unnamed x7, local copies, waits for them, and re-layouts  6.61 us

profile of v5, /device:TPU:112, one launch (start us, length us, event | category | flops | bytes accessed | tf_op | source)
XLA Modules:
  0.0 258.3 jit_solution(2563842836366683181)
XLA Ops:
  0.6 251.1 %shard_map.76 = (bf16[1,640,1536]{2,1,0:T(8,128)(2,1)}, bf16[1,640,1536]{2,1,0:T(8,128)(2,1)}, bf16[1,1536,640]{2,1,0:T(8,128)(2,1)}, f32[16,2,512,1536]{3,2,1,0:T(8,128)}, bf16[16,512,1536]{2,1,0:T(8,128)(2,1)}) custom-call(bf16[16,512,640]{2,1,0:T(8,128)(2,1)} %x_hbm.1, bf16[16,512,640]{2,1,0:T(8,128)(2,1)} %dy_hbm.1, bf16[1,640,1536]{2,1,0:T(8,128)(2,1)} %wg_hbm.1, ...), custom_call_target="tpu_custom_call" | custom-call | tf_op jit(solution)/shard_map/pallas_call | solution.py:372
  251.7 0.0 copy-start.1
  251.7 3.1 %copy.11 = bf16[1,640,1536]{2,1,0:T(8,128)(2,1)} copy(bf16[1,640,1536]{2,1,0:T(8,128)(2,1)} %get-tuple-element.12) | data formatting | bytes 3932160
  254.8 0.0 copy-done.1
  254.8 0.0 copy-start
  254.8 1.3 copy.12
  256.1 1.0 copy-done
  257.1 1.3 copy.13
Async XLA Ops:
  251.7 3.1 %copy-start.1 = (bf16[1,640,1536]{2,1,0:T(8,128)(2,1)S(1)}, bf16[1,640,1536]{2,1,0:T(8,128)(2,1)}, u32[]{:S(2)}) copy-start(bf16[1,640,1536]{2,1,0:T(8,128)(2,1)} %get-tuple-element.13) | copy-start | bytes 5898244
  254.8 2.3 copy-start
